TPU v7x, 32 devices: a whole 2x2x4 slice. The times are simulated.
32 devices in a mesh: dp: 4 (over x, core), seq: 4 (over z), tensor: 2 (over y).
Axes of the slice: x: 2, y: 2, z: 4, core: 2. Of those that a mesh axis runs over, the one named last changes fastest.
Arguments:
- vit_out: bfloat16 [4096, 3200], P(('dp', 'seq')), may hold values from -6 to 6
- ln_gain: float32 [3200], replicated, may hold values from 0.1 to 1.9
- ln_bias: float32 [3200], replicated, may hold values from -3 to 3
- proj_weight: bfloat16 [3200, 4, 2048], P(None, None, 'tensor'), may hold values from -0.109375 to 0.109375
- proj_bias: float32 [4, 2048], P(None, 'tensor'), may hold values from -3 to 3
- text_embed: bfloat16 [16384, 8192], P('dp', ('seq', 'tensor')), may hold values from -6 to 6
- norm_gain: float32 [8192], P(('seq', 'tensor')), may hold values from 0.1 to 1.9
- tile_dest: int32 [32, 1], replicated, may hold values from 0 to 3; in each aligned block of 8 rows (0 to 7, 8 to 15, ...) at most 4 rows name the same one
- tile_place: int32 [4, 32], replicated, may hold values from 0 to 31, each once within a row
Outputs:
- normed: bfloat16 [16384, 8192], P('dp', ('seq', 'tensor'))
Inputs may be any that keep to these rules, and one draw needn't show every extreme that they name: `tile_dest`: in each aligned block of 8 rows (one encoder group's tiles) no replica is named more than 4 times, a bound that some block reaches. `tile_place`: each row is a permutation of 0 to 31.
All inputs are finite; a program needn't handle non-finite values.
Results may differ from a plain program's by a relative error of at most 0.0048.
Values may be sent and summed in bfloat16 or wider, within the bound.
A program may use at most 128 MiB of HBM per device.

v0:
```python
import jax
import jax.numpy as jnp
from jax import lax
from jax.sharding import PartitionSpec as P

D = 8192
TILE = 128


def layer_norm(rows, ln_gain, ln_bias):
    values = rows.astype(jnp.float32)
    center = values - jnp.mean(values, axis=-1, keepdims=True)
    spread = jnp.mean(center * center, axis=-1, keepdims=True)
    return (center * lax.rsqrt(spread + 1e-06) * ln_gain + ln_bias).astype(jnp.bfloat16)


def arrival_ranks(destination, replicas):
    onehot = (destination[:, None] == jnp.arange(replicas, dtype=jnp.int32)[None, :]).astype(
        jnp.int32
    )
    before = jnp.cumsum(onehot, axis=0) - onehot
    return jnp.sum(before * onehot, axis=1)


def row_squares(rows):
    values = rows.astype(jnp.float32)
    return jnp.sum(values * values, axis=-1)


def local(
    vit_out, ln_gain, ln_bias, proj_weight, proj_bias, text_embed, norm_gain, tile_dest, tile_place
):
    replicas = lax.axis_size("dp")
    owners = lax.axis_size("seq")
    my_replica = lax.axis_index("dp")
    local_rows = vit_out.shape[0]
    width_in = vit_out.shape[1]
    column_block = proj_weight.shape[2]
    positions = tile_place.shape[1]
    seq_rows = text_embed.shape[0]
    group_tiles = owners * local_rows // TILE
    total_tiles = tile_dest.shape[0]
    normed_in = layer_norm(vit_out, ln_gain, ln_bias)
    weights_flat = proj_weight.reshape(width_in, owners * column_block)
    hidden = jnp.dot(
        normed_in, weights_flat, preferred_element_type=jnp.float32
    ) + proj_bias.reshape(-1)
    projected = hidden.astype(jnp.bfloat16)
    regrouped = lax.all_to_all(
        projected.reshape(local_rows, owners, column_block),
        "seq",
        split_axis=1,
        concat_axis=0,
        tiled=True,
    )
    group_rows = regrouped.reshape(owners * local_rows, column_block)
    destination = tile_dest[:, 0]
    ranks = arrival_ranks(destination, replicas)
    place_row = lax.dynamic_index_in_dim(tile_place, my_replica, 0, keepdims=False)
    slot_of_tile = jnp.where(
        destination == my_replica, jnp.take(place_row, jnp.minimum(ranks, positions - 1)), -1
    )
    matches = slot_of_tile[None, :] == jnp.arange(positions, dtype=jnp.int32)[:, None]
    source_tile = (
        jnp.sum(
            matches.astype(jnp.int32) * (jnp.arange(total_tiles, dtype=jnp.int32) + 1)[None, :],
            axis=1,
        )
        - 1
    )
    text_tiles = text_embed.reshape(positions, TILE, column_block)
    capacity = max(2, 2 * group_tiles // replicas)
    local_dest = lax.dynamic_slice_in_dim(destination, my_replica * group_tiles, group_tiles)
    local_rank = arrival_ranks(local_dest, replicas)
    slot_index = local_dest * capacity + local_rank
    filling = slot_index[None, :] == jnp.arange(replicas * capacity, dtype=jnp.int32)[:, None]
    slot_source = (
        jnp.sum(
            filling.astype(jnp.int32) * (jnp.arange(group_tiles, dtype=jnp.int32) + 1)[None, :],
            axis=1,
        )
        - 1
    )
    tiles = group_rows.reshape(group_tiles, TILE, column_block)
    outgoing = jnp.where(
        (slot_source >= 0)[:, None, None],
        tiles[jnp.clip(slot_source, 0, group_tiles - 1)],
        jnp.zeros((), jnp.bfloat16),
    )
    outgoing = outgoing.reshape(replicas, capacity, TILE, column_block)
    incoming = lax.all_to_all(outgoing, "dp", split_axis=0, concat_axis=0, tiled=True).reshape(
        replicas * capacity, TILE, column_block
    )
    group_ranks = jax.vmap(lambda block: arrival_ranks(block, replicas))(
        destination.reshape(replicas, group_tiles)
    ).reshape(-1)
    safe_tile = jnp.clip(source_tile, 0, total_tiles - 1)
    arrival_index = safe_tile // group_tiles * capacity + jnp.take(group_ranks, safe_tile)
    picked = incoming[jnp.clip(arrival_index, 0, replicas * capacity - 1)]
    assembled = jnp.where((source_tile >= 0)[:, None, None], picked, text_tiles).reshape(
        seq_rows, column_block
    )
    squares = row_squares(assembled)
    totals = lax.psum(squares, ("seq", "tensor"))
    scale = lax.rsqrt(totals / D + 1e-05)
    return (assembled.astype(jnp.float32) * scale[:, None] * norm_gain).astype(jnp.bfloat16)


def solution(mesh):
    placed = (
        P(("dp", "seq"), None),
        P(),
        P(),
        P(None, None, "tensor"),
        P(None, "tensor"),
        P("dp", ("seq", "tensor")),
        P(("seq", "tensor")),
        P(),
        P(),
    )
    return jax.shard_map(
        local, mesh=mesh, in_specs=placed, out_specs=P("dp", ("seq", "tensor")), check_vma=False
    )
```

profile of v0, /device:TPU:0, one launch (start us, length us, event | category | flops | bytes accessed | tf_op | source)
XLA Modules:
  0.0 208.5 jit_solution(405158420390305600)
XLA Ops:
  0.0 0.0 copy-start
  0.0 0.0 copy-start.2
  0.0 0.0 copy-start.1
  0.0 0.0 copy-start.5
  0.0 0.0 copy-start.6
  0.0 18.2 %copy.13 = bf16[400,8,4,1024]{3,1,2,0:T(8,128)(2,1)} copy(bf16[400,8,4,1024]{3,2,1,0:T(4,128)(2,1)} %bitcast.39) | data formatting | bytes 52428800
  18.2 0.0 copy-done.2
  18.2 0.0 copy-done.1
  18.3 0.3 convert_reduce_fusion
  18.6 0.6 fusion.6
  19.2 0.0 copy-done.5
  19.2 0.0 copy-done.6
  19.2 12.3 %fusion.3 = bf16[256,4096]{1,0:T(8,128)(2,1)S(1)} fusion(bf16[3200,4096]{1,0:T(8,128)(2,1)} %bitcast.40, f32[4096]{0:T(1024)S(1)} %bitcast.46, bf16[256,3200]{1,0:T(8,128)(2,1)S(1)} %copy-done.1, f32[3200]{0:T(1024)S(1)} %copy-done.5, f32[3200]{0:T(1024)S(1)} %copy-done.6, f32[256]{0:T(256)S(1)} %add_rsqrt_fusion.1, f32[256]{0:T(256)S(1)} %broadcast_multiply_fusion), kind=kOutput, calls=%fused_computation.11 | convolution fusion | flops 6717898752 | bytes 29993984 | tf_op jit(solution)/shard_map/dot_general | solution.py:45
  31.5 0.0 copy-start.3
  31.5 1.5 copy.17
  33.0 6.4 %all-to-all-start = ((bf16[256,4,1024]{2,0,1:T(8,128)(2,1)}), bf16[256,4,1024]{2,0,1:T(8,128)(2,1)S(1)}, u32[]{:S(2)}, u32[]{:S(2)}) async-start(bf16[256,4,1024]{2,0,1:T(8,128)(2,1)} %bitcast.43), calls=%async_computation | async-start | bytes 4194304 | tf_op jit(solution)/shard_map/all_to_all | solution.py:49
  39.4 0.0 copy-done.3
  39.4 0.1 dynamic-slice_bitcast_fusion
  39.5 0.2 reduce_window_sum.34
  39.7 0.1 iota_add_fusion
  39.8 0.1 select_reduce_fusion.3
  39.9 0.1 ge.24
  40.0 47.6 %all-to-all-done = bf16[256,4,1024]{2,0,1:T(8,128)(2,1)S(1)} async-done(((bf16[256,4,1024]{2,0,1:T(8,128)(2,1)}), bf16[256,4,1024]{2,0,1:T(8,128)(2,1)S(1)}, u32[]{:S(2)}, u32[]{:S(2)}) %all-to-all-start) | async-done | bytes 2097184 | tf_op jit(solution)/shard_map/all_to_all | solution.py:49
  87.6 2.8 %gather_fusion = bf16[16,128,1024]{2,1,0:T(8,128)(2,1)} fusion(bf16[8,128,1024]{2,1,0:T(8,128)(2,1)S(1)} %bitcast.41, s32[1024]{0:T(1024)S(1)} %pad_clamp_fusion.2), kind=kCustom, calls=%fused_computation.2 | custom fusion | bytes 8388672 | tf_op jit(solution)/shard_map/gather | solution.py:87
  90.4 4.5 %broadcast_select_fusion = bf16[4,4,128,1024]{3,2,1,0:T(8,128)(2,1)} fusion(bf16[4,4,128,1024]{3,2,1,0:T(8,128)(2,1)} %bitcast.42, pred[4,4]{1,0:T(4,128)(4,1)S(1)} %ge.24), kind=kLoop, calls=%fused_computation.12 | loop fusion | flops 2097152 | bytes 8388624 | tf_op jit(solution)/shard_map/jit(_where)/select_n | solution.py:85
  95.0 4.9 %all-to-all-start.1 = ((bf16[4,4,128,1024]{3,2,1,0:T(8,128)(2,1)}), bf16[4,4,128,1024]{3,2,1,0:T(8,128)(2,1)}, u32[]{:S(2)}, u32[]{:S(2)}) async-start(bf16[4,4,128,1024]{3,2,1,0:T(8,128)(2,1)} %broadcast_select_fusion), calls=%async_computation.1 | async-start | bytes 8388608 | tf_op jit(solution)/shard_map/all_to_all | solution.py:91
  99.9 0.6 broadcast.200
  100.5 0.7 reduce.3
  101.2 0.1 eq.87
  101.3 0.7 reduce_window_sum.35
  102.0 0.1 reshape.103
  102.1 0.1 fusion.15
  102.2 0.1 reduce_window_sum.33
  102.2 0.0 copy-done
  102.3 0.2 select_reduce_fusion.1
  102.5 0.7 gather_fusion.2
  103.2 0.1 select_reduce_fusion
  103.3 0.7 gather_fusion.3
  104.1 0.1 broadcast_bitcast_fusion
  104.1 43.9 %all-to-all-done.1 = bf16[4,4,128,1024]{3,2,1,0:T(8,128)(2,1)} async-done(((bf16[4,4,128,1024]{3,2,1,0:T(8,128)(2,1)}), bf16[4,4,128,1024]{3,2,1,0:T(8,128)(2,1)}, u32[]{:S(2)}, u32[]{:S(2)}) %all-to-all-start.1) | async-done | bytes 4194336 | tf_op jit(solution)/shard_map/all_to_all | solution.py:91
  148.1 7.1 %gather_fusion.1 = bf16[32,128,1024]{2,1,0:T(8,128)(2,1)} fusion(bf16[16,128,1024]{2,1,0:T(8,128)(2,1)} %bitcast.10, s32[1024]{0:T(1024)S(1)} %pad_clamp_fusion), kind=kCustom, calls=%fused_computation.3 | custom fusion | bytes 16777344 | tf_op jit(solution)/shard_map/gather | solution.py:99
  155.2 0.0 copy-start.4
  155.2 7.7 %fusion = f32[4096]{0:T(1024)S(1)} fusion(bf16[4096,1024]{1,0:T(8,128)(2,1)} %param.16, bf16[32,128,1024]{2,1,0:T(8,128)(2,1)} %gather_fusion.1, pred[4096]{0:T(1024)(128)(4,1)S(1)} %broadcast_bitcast_fusion), kind=kLoop, calls=%fused_computation.6 | loop fusion | flops 16773120 | bytes 16797696 | tf_op jit(solution)/shard_map/reduce_sum | solution.py:27
  162.9 35.3 %psum.7 = f32[4096]{0:T(1024)S(1)} all-reduce(f32[4096]{0:T(1024)S(1)} %fusion), channel_id=1, replica_groups=mesh['dp'=4,'seq'=4,'tensor'=2] {'seq','tensor'}, use_global_device_ids=true, to_apply=%region_11.13 | all-reduce | flops 4096 | bytes 32768 | tf_op jit(solution)/shard_map/psum | solution.py:104
  198.2 0.0 copy-done.4
  198.2 10.2 %fusion.2 = bf16[4096,1024]{1,0:T(8,128)(2,1)} fusion(f32[1024]{0:T(1024)S(1)} %copy-done.4, f32[4096]{0:T(1024)S(1)} %add_rsqrt_fusion, bf16[4096,1024]{1,0:T(8,128)(2,1)} %param.16, bf16[32,128,1024]{2,1,0:T(8,128)(2,1)} %gather_fusion.1, pred[4096]{0:T(1024)(128)(4,1)S(1)} %broadcast_bitcast_fusion), kind=kLoop, calls=%fused_computation.8 | loop fusion | flops 20971520 | bytes 25190400 | tf_op jit(solution)/shard_map/convert_element_type | solution.py:106
  (20 shorter events, 0.2 us)
Async XLA Ops:
  0.0 102.2 %copy-start = (s32[4,32]{1,0:T(4,128)S(1)}, s32[4,32]{1,0:T(4,128)}, u32[]{:S(2)}) copy-start(s32[4,32]{1,0:T(4,128)} %param.19) | copy-start | bytes 1540
  0.0 18.2 %copy-start.2 = (f32[4,1024]{1,0:T(4,128)S(1)}, f32[4,1024]{1,0:T(4,128)}, u32[]{:S(2)}) copy-start(f32[4,1024]{1,0:T(4,128)} %param.15) | copy-start | bytes 49156
  0.0 18.2 %copy-start.1 = (bf16[256,3200]{1,0:T(8,128)(2,1)S(1)}, bf16[256,3200]{1,0:T(8,128)(2,1)}, u32[]{:S(2)}) copy-start(bf16[256,3200]{1,0:T(8,128)(2,1)} %param.11) | copy-start | bytes 4915204
  0.0 19.1 %copy-start.5 = (f32[3200]{0:T(1024)S(1)}, f32[3200]{0:T(1024)}, u32[]{:S(2)}) copy-start(f32[3200]{0:T(1024)} %param.13) | copy-start | bytes 38404
  0.0 19.2 %copy-start.6 = (f32[3200]{0:T(1024)S(1)}, f32[3200]{0:T(1024)}, u32[]{:S(2)}) copy-start(f32[3200]{0:T(1024)} %param.12) | copy-start | bytes 38404
  31.5 7.9 %copy-start.3 = (s32[32,1]{0,1:T(1,128)S(1)}, s32[32,1]{0,1:T(1,128)}, u32[]{:S(2)}) copy-start(s32[32,1]{0,1:T(1,128)} %param.18) | copy-start | bytes 388
  33.0 54.6 %all-to-all-start = ((bf16[256,4,1024]{2,0,1:T(8,128)(2,1)}), bf16[256,4,1024]{2,0,1:T(8,128)(2,1)S(1)}, u32[]{:S(2)}, u32[]{:S(2)}) async-start(bf16[256,4,1024]{2,0,1:T(8,128)(2,1)} %bitcast.43), calls=%async_computation | async-start | bytes 4194304 | tf_op jit(solution)/shard_map/all_to_all | solution.py:49
  95.0 53.1 %all-to-all-start.1 = ((bf16[4,4,128,1024]{3,2,1,0:T(8,128)(2,1)}), bf16[4,4,128,1024]{3,2,1,0:T(8,128)(2,1)}, u32[]{:S(2)}, u32[]{:S(2)}) async-start(bf16[4,4,128,1024]{3,2,1,0:T(8,128)(2,1)} %broadcast_select_fusion), calls=%async_computation.1 | async-start | bytes 8388608 | tf_op jit(solution)/shard_map/all_to_all | solution.py:91
  155.2 43.0 %copy-start.4 = (f32[1024]{0:T(1024)S(1)}, f32[1024]{0:T(1024)}, u32[]{:S(2)}) copy-start(f32[1024]{0:T(1024)} %param.17) | copy-start | bytes 12292
where the time goes:
time: 209 us; the launch traced here: 208 us
  waiting for transfers between devices  91.6 us (44%)
  blocking collectives  35.3 us (17%)
  local copies, waits for them, and re-layouts  32.1 us (15%)
  other arithmetic  25.8 us (12%)
  matrix products  12.3 us (6%)
  starting transfers between devices  11.3 us (5%)
    all_to_all x1, waiting for transfers between devices, local(): lax.all_to_all(projected.reshape(local_rows, owners, column_block), 'seq'...  47.6 us
    all_to_all x1, waiting for transfers between devices, local(): lax.all_to_all(outgoing, 'dp', split_axis=0, concat_axis=0, tiled=True)  43.9 us
    psum x1, blocking collectives, local(): totals = lax.psum(squares, ('seq', 'tensor'))  35.3 us
    unnamed x17, local copies, waits for them, and re-layouts  18.8 us
    dot_general x1, matrix products, local(): jnp.dot(normed_in, weights_flat, preferred_element_type=jnp.float32)  12.3 us
    convert_element_type x1, other arithmetic, local(): (assembled.astype(jnp.float32) * scale[:, None] * norm_gain).astype(jnp.b...  10.2 us
    reduce_sum x1, other arithmetic, row_squares(): return jnp.sum(values * values, axis=-1)  7.74 us
    gather x1, local copies, waits for them, and re-layouts, local(): picked = incoming[jnp.clip(arrival_index, 0, replicas * capacity - 1)]  7.11 us
  transfers between devices with their start and end apart: 2, of which 2 were waited for; matrix products, arithmetic and copies ran while one was open for 2% of the time, Pallas kernels for 0%

commit v1 on v0

--- a/solution.py
+++ b/solution.py
@@ -101,7 +101,7 @@
         seq_rows, column_block
     )
     squares = row_squares(assembled)
-    totals = lax.psum(squares, ("seq", "tensor"))
+    totals = jnp.sum(lax.all_gather(squares, ("seq", "tensor")), axis=0)
     scale = lax.rsqrt(totals / D + 1e-05)
     return (assembled.astype(jnp.float32) * scale[:, None] * norm_gain).astype(jnp.bfloat16)
 

time: 209 us -> 204 us (0.976)
  blocking collectives: 35.3 us -> 30.5 us
    psum x1 -> x0, blocking collectives: 35.3 us -> none  [local(): totals = lax.psum(squares, ('seq', 'tensor'))]
    all_gather x0 -> x1, blocking collectives: none -> 30.5 us  [local(): totals = jnp.sum(lax.all_gather(squares, ('seq', 'tensor')), axis=0)]
where the time goes in v1:
time: 204 us
  waiting for transfers between devices  91.6 us (45%)
  local copies, waits for them, and re-layouts  32.1 us (16%)
  blocking collectives  30.5 us (15%)
  other arithmetic  25.8 us (13%)
  matrix products  12.3 us (6%)
  starting transfers between devices  11.3 us (6%)
    all_to_all x1, waiting for transfers between devices, local(): lax.all_to_all(projected.reshape(local_rows, owners, column_block), 'seq'...  47.6 us
    all_to_all x1, waiting for transfers between devices, local(): lax.all_to_all(outgoing, 'dp', split_axis=0, concat_axis=0, tiled=True)  43.9 us
    all_gather x1, blocking collectives, local(): totals = jnp.sum(lax.all_gather(squares, ('seq', 'tensor')), axis=0)  30.5 us
    unnamed x17, local copies, waits for them, and re-layouts  18.8 us
    dot_general x1, matrix products, local(): jnp.dot(normed_in, weights_flat, preferred_element_type=jnp.float32)  12.3 us
    convert_element_type x1, other arithmetic, local(): (assembled.astype(jnp.float32) * scale[:, None] * norm_gain).astype(jnp.b...  10.2 us
    reduce_sum x1, other arithmetic, row_squares(): return jnp.sum(values * values, axis=-1)  7.74 us
    gather x1, local copies, waits for them, and re-layouts, local(): picked = incoming[jnp.clip(arrival_index, 0, replicas * capacity - 1)]  7.11 us
  transfers between devices with their start and end apart: 2, of which 2 were waited for; matrix products, arithmetic and copies ran while one was open for 2% of the time, Pallas kernels for 0%

profile of v1, /device:TPU:0, one launch (start us, length us, event | category | flops | bytes accessed | tf_op | source)
XLA Modules:
  0.0 203.8 jit_solution(11748659698741573480)
XLA Ops:
  0.0 0.0 copy-start
  0.0 0.0 copy-start.2
  0.0 0.0 copy-start.1
  0.0 0.0 copy-start.5
  0.0 0.0 copy-start.6
  0.0 18.2 %copy.14 = bf16[400,8,4,1024]{3,1,2,0:T(8,128)(2,1)} copy(bf16[400,8,4,1024]{3,2,1,0:T(4,128)(2,1)} %bitcast.39) | data formatting | bytes 52428800
  18.2 0.0 copy-done.2
  18.2 0.0 copy-done.1
  18.3 0.3 convert_reduce_fusion
  18.6 0.6 fusion.6
  19.2 0.0 copy-done.5
  19.2 0.0 copy-done.6
  19.2 12.3 %fusion.3 = bf16[256,4096]{1,0:T(8,128)(2,1)S(1)} fusion(bf16[3200,4096]{1,0:T(8,128)(2,1)} %bitcast.40, f32[4096]{0:T(1024)S(1)} %bitcast.46, bf16[256,3200]{1,0:T(8,128)(2,1)S(1)} %copy-done.1, f32[3200]{0:T(1024)S(1)} %copy-done.5, f32[3200]{0:T(1024)S(1)} %copy-done.6, f32[256]{0:T(256)S(1)} %add_rsqrt_fusion.1, f32[256]{0:T(256)S(1)} %broadcast_multiply_fusion), kind=kOutput, calls=%fused_computation.11 | convolution fusion | flops 6717898752 | bytes 29993984 | tf_op jit(solution)/shard_map/dot_general | solution.py:45
  31.5 0.0 copy-start.3
  31.5 1.5 copy.18
  33.0 6.4 %all-to-all-start = ((bf16[256,4,1024]{2,0,1:T(8,128)(2,1)}), bf16[256,4,1024]{2,0,1:T(8,128)(2,1)S(1)}, u32[]{:S(2)}, u32[]{:S(2)}) async-start(bf16[256,4,1024]{2,0,1:T(8,128)(2,1)} %bitcast.43), calls=%async_computation | async-start | bytes 4194304 | tf_op jit(solution)/shard_map/all_to_all | solution.py:49
  39.4 0.0 copy-done.3
  39.4 0.1 dynamic-slice_bitcast_fusion
  39.5 0.2 reduce_window_sum.34
  39.7 0.1 iota_add_fusion
  39.8 0.1 select_reduce_fusion.3
  39.9 0.1 ge.24
  40.0 47.6 %all-to-all-done = bf16[256,4,1024]{2,0,1:T(8,128)(2,1)S(1)} async-done(((bf16[256,4,1024]{2,0,1:T(8,128)(2,1)}), bf16[256,4,1024]{2,0,1:T(8,128)(2,1)S(1)}, u32[]{:S(2)}, u32[]{:S(2)}) %all-to-all-start) | async-done | bytes 2097184 | tf_op jit(solution)/shard_map/all_to_all | solution.py:49
  87.6 2.8 %gather_fusion = bf16[16,128,1024]{2,1,0:T(8,128)(2,1)} fusion(bf16[8,128,1024]{2,1,0:T(8,128)(2,1)S(1)} %bitcast.41, s32[1024]{0:T(1024)S(1)} %pad_clamp_fusion.2), kind=kCustom, calls=%fused_computation.2 | custom fusion | bytes 8388672 | tf_op jit(solution)/shard_map/gather | solution.py:87
  90.4 4.5 %broadcast_select_fusion = bf16[4,4,128,1024]{3,2,1,0:T(8,128)(2,1)} fusion(bf16[4,4,128,1024]{3,2,1,0:T(8,128)(2,1)} %bitcast.42, pred[4,4]{1,0:T(4,128)(4,1)S(1)} %ge.24), kind=kLoop, calls=%fused_computation.12 | loop fusion | flops 2097152 | bytes 8388624 | tf_op jit(solution)/shard_map/jit(_where)/select_n | solution.py:85
  95.0 4.9 %all-to-all-start.1 = ((bf16[4,4,128,1024]{3,2,1,0:T(8,128)(2,1)}), bf16[4,4,128,1024]{3,2,1,0:T(8,128)(2,1)}, u32[]{:S(2)}, u32[]{:S(2)}) async-start(bf16[4,4,128,1024]{3,2,1,0:T(8,128)(2,1)} %broadcast_select_fusion), calls=%async_computation.1 | async-start | bytes 8388608 | tf_op jit(solution)/shard_map/all_to_all | solution.py:91
  99.9 0.6 broadcast.207
  100.5 0.7 reduce.3
  101.2 0.1 eq.87
  101.3 0.7 reduce_window_sum.35
  102.0 0.1 reshape.107
  102.1 0.1 fusion.15
  102.2 0.1 reduce_window_sum.33
  102.2 0.0 copy-done
  102.3 0.2 select_reduce_fusion.1
  102.5 0.7 gather_fusion.2
  103.2 0.1 select_reduce_fusion
  103.3 0.7 gather_fusion.3
  104.1 0.1 broadcast_bitcast_fusion
  104.1 43.9 %all-to-all-done.1 = bf16[4,4,128,1024]{3,2,1,0:T(8,128)(2,1)} async-done(((bf16[4,4,128,1024]{3,2,1,0:T(8,128)(2,1)}), bf16[4,4,128,1024]{3,2,1,0:T(8,128)(2,1)}, u32[]{:S(2)}, u32[]{:S(2)}) %all-to-all-start.1) | async-done | bytes 4194336 | tf_op jit(solution)/shard_map/all_to_all | solution.py:91
  148.1 7.1 %gather_fusion.1 = bf16[32,128,1024]{2,1,0:T(8,128)(2,1)} fusion(bf16[16,128,1024]{2,1,0:T(8,128)(2,1)} %bitcast.10, s32[1024]{0:T(1024)S(1)} %pad_clamp_fusion), kind=kCustom, calls=%fused_computation.3 | custom fusion | bytes 16777344 | tf_op jit(solution)/shard_map/gather | solution.py:99
  155.2 0.0 copy-start.4
  155.2 7.7 %fusion = f32[4096]{0:T(1024)S(1)} fusion(bf16[4096,1024]{1,0:T(8,128)(2,1)} %param.16, bf16[32,128,1024]{2,1,0:T(8,128)(2,1)} %gather_fusion.1, pred[4096]{0:T(1024)(128)(4,1)S(1)} %broadcast_bitcast_fusion), kind=kLoop, calls=%fused_computation.6 | loop fusion | flops 16773120 | bytes 16797696 | tf_op jit(solution)/shard_map/reduce_sum | solution.py:27
  162.9 30.5 %all-gather = f32[32768]{0:T(1024)S(1)} all-gather(f32[4096]{0:T(1024)S(1)} %fusion), channel_id=2, replica_groups=mesh['dp'=4,'seq'=4,'tensor'=2] {'seq','tensor'}, dimensions={0}, use_global_device_ids=true | all-gather | bytes 147456 | tf_op jit(solution)/shard_map/all_gather | solution.py:104
  193.6 0.0 copy-done.4
  193.6 10.2 %fusion.2 = bf16[4096,1024]{1,0:T(8,128)(2,1)} fusion(f32[1024]{0:T(1024)S(1)} %copy-done.4, f32[4096]{0:T(1024)S(1)} %add_rsqrt_fusion, bf16[4096,1024]{1,0:T(8,128)(2,1)} %param.16, bf16[32,128,1024]{2,1,0:T(8,128)(2,1)} %gather_fusion.1, pred[4096]{0:T(1024)(128)(4,1)S(1)} %broadcast_bitcast_fusion), kind=kLoop, calls=%fused_computation.8 | loop fusion | flops 20971520 | bytes 25190400 | tf_op jit(solution)/shard_map/convert_element_type | solution.py:106
  (22 shorter events, 0.3 us)
Async XLA Ops:
  0.0 102.2 %copy-start = (s32[4,32]{1,0:T(4,128)S(1)}, s32[4,32]{1,0:T(4,128)}, u32[]{:S(2)}) copy-start(s32[4,32]{1,0:T(4,128)} %param.19) | copy-start | bytes 1540
  0.0 18.2 %copy-start.2 = (f32[4,1024]{1,0:T(4,128)S(1)}, f32[4,1024]{1,0:T(4,128)}, u32[]{:S(2)}) copy-start(f32[4,1024]{1,0:T(4,128)} %param.15) | copy-start | bytes 49156
  0.0 18.2 %copy-start.1 = (bf16[256,3200]{1,0:T(8,128)(2,1)S(1)}, bf16[256,3200]{1,0:T(8,128)(2,1)}, u32[]{:S(2)}) copy-start(bf16[256,3200]{1,0:T(8,128)(2,1)} %param.11) | copy-start | bytes 4915204
  0.0 19.1 %copy-start.5 = (f32[3200]{0:T(1024)S(1)}, f32[3200]{0:T(1024)}, u32[]{:S(2)}) copy-start(f32[3200]{0:T(1024)} %param.13) | copy-start | bytes 38404
  0.0 19.2 %copy-start.6 = (f32[3200]{0:T(1024)S(1)}, f32[3200]{0:T(1024)}, u32[]{:S(2)}) copy-start(f32[3200]{0:T(1024)} %param.12) | copy-start | bytes 38404
  31.5 7.9 %copy-start.3 = (s32[32,1]{0,1:T(1,128)S(1)}, s32[32,1]{0,1:T(1,128)}, u32[]{:S(2)}) copy-start(s32[32,1]{0,1:T(1,128)} %param.18) | copy-start | bytes 388
  33.0 54.6 %all-to-all-start = ((bf16[256,4,1024]{2,0,1:T(8,128)(2,1)}), bf16[256,4,1024]{2,0,1:T(8,128)(2,1)S(1)}, u32[]{:S(2)}, u32[]{:S(2)}) async-start(bf16[256,4,1024]{2,0,1:T(8,128)(2,1)} %bitcast.43), calls=%async_computation | async-start | bytes 4194304 | tf_op jit(solution)/shard_map/all_to_all | solution.py:49
  95.0 53.1 %all-to-all-start.1 = ((bf16[4,4,128,1024]{3,2,1,0:T(8,128)(2,1)}), bf16[4,4,128,1024]{3,2,1,0:T(8,128)(2,1)}, u32[]{:S(2)}, u32[]{:S(2)}) async-start(bf16[4,4,128,1024]{3,2,1,0:T(8,128)(2,1)} %broadcast_select_fusion), calls=%async_computation.1 | async-start | bytes 8388608 | tf_op jit(solution)/shard_map/all_to_all | solution.py:91
  155.2 38.4 %copy-start.4 = (f32[1024]{0:T(1024)S(1)}, f32[1024]{0:T(1024)}, u32[]{:S(2)}) copy-start(f32[1024]{0:T(1024)} %param.17) | copy-start | bytes 12292
